TPU v7x, 256 devices: a 8x8x2 block of a 8x8x16 slice. The times are simulated.
256 devices in a mesh: groups: 2 (over z), seq: 64 (over x, y), mp: 2 (over core).
Axes of the slice: x: 8, y: 8, z: 2, core: 2. Of those that a mesh axis runs over, the one named last changes fastest.
The devices are a block of a 8x8x16 slice.
Arguments:
- latent_cache: bfloat16 [16384, 64, 512], P(('groups', 'seq')), parts along dimension 0, may hold values from -6 to 6
- rope_cache: bfloat16 [16384, 4096], P(('groups', 'seq')), parts along dimension 0, may hold values from -6 to 6
- q_nope: bfloat16 [16, 128, 128], P('groups', 'mp'), parts along dimension 0, may hold values from -12 to 12
- q_rope: bfloat16 [16, 128, 64], P('groups', 'mp'), parts along dimension 0, may hold values from -2000 to 2000
- w_uk: bfloat16 [128, 128, 512], P('mp', None, 'seq'), may hold values from -0.5 to 0.5
- value_up_weight: bfloat16 [128, 512, 128], P('mp', 'seq'), may hold values from -0.25 to 0.25
- w_out: bfloat16 [16384, 7168], P('mp', 'seq'), may hold values from -0.046875 to 0.046875
- page_table: int32 [16, 2048], P('groups'), parts along dimension 0, may hold values from 0 to 8191, as said below
- lengths: int32 [16], P('groups'), parts along dimension 0, may hold values from 16384 to 131072, as said below
Outputs:
- output: bfloat16 [16, 7168], P('groups', ('seq', 'mp')), parts along dimension 0
There are 2 independent parts, one for each index of `groups`. A program takes and returns all parts, laid end to end along the dimension named above; an argument that names none is the same for every part. Nothing has to cross between parts.
Inputs may be any that keep to these rules, and one draw needn't show every extreme that they name: `lengths`: every sequence has one eighth of 131072 tokens or more; the longest has exactly 131072. page_table[b,p] for p < ceil(lengths[b] / 64) is the global slot (shard index times 128 plus local slot) holding that page; these live entries are all distinct; the other entries are 0 and unused.
All inputs are finite; a program needn't handle non-finite values.
Results may differ from a plain program's by a relative error of at most 0.012.
Values may be sent and summed in bfloat16 or wider, within the bound.
A program may use at most 64 MiB of HBM per device.

v0:
```python
import jax
import jax.numpy as jnp
from jax import lax
from jax.sharding import Mesh
from jax.sharding import PartitionSpec as P

SEQ = ("seq_0", "seq_1")
GROUPS_SEQ = ("groups", "seq_0", "seq_1")
SEQ_MP = ("seq_0", "seq_1", "mp")


NEG = -1e30


def laid_out(tiles, dim):
    tiles = jnp.moveaxis(tiles, 0, dim)
    lengths = tiles.shape
    return tiles.reshape(*lengths[:dim], lengths[dim] * lengths[dim + 1], *lengths[dim + 2 :])


def from_everyone(x, axis):
    size = lax.axis_size(axis)
    return lax.all_to_all(jnp.broadcast_to(x[None], (size, *x.shape)), axis, 0, 0, tiled=True)


def collect(x, axis, dim):
    return laid_out(from_everyone(x, axis), dim)


def side_by_side(arrays, axis, split_dim, concat_dim, along):
    ends, at = ([], 0)
    for a in arrays[:-1]:
        at += a.shape[along]
        ends.append(at)
    both = jnp.concatenate(arrays, axis=along)
    return tuple(
        jnp.split(
            lax.all_to_all(both, axis, split_axis=split_dim, concat_axis=concat_dim, tiled=True),
            ends,
            axis=along,
        )
    )


def by_axis(x, axes):
    for axis in axes:
        x = lax.psum(x, axis)
    return x


def cut_along(x, dim, size):
    lengths = x.shape
    tiles = x.reshape(*lengths[:dim], size, lengths[dim] // size, *lengths[dim + 1 :])
    return jnp.moveaxis(tiles, dim, 0)


def sum_at_owner(x, axis, dim):
    size = lax.axis_size(axis)
    tiles = lax.all_to_all(cut_along(x, dim, size), axis, 0, 0, tiled=True)
    return jnp.sum(tiles, axis=0)


def local(
    latent_cache, rope_cache, q_nope, q_rope, w_uk, value_up_weight, w_out, page_table, lengths
):
    slots_dev, page_len, latent_width = latent_cache.shape
    rope_width = q_rope.shape[2]
    seq_count, heads = (q_nope.shape[0], q_nope.shape[1])
    score_scale = (q_nope.shape[2] + rope_width) ** (-0.5)
    q_part = jnp.einsum("bhn,hnk->bhk", q_nope, w_uk, preferred_element_type=jnp.float32).astype(
        jnp.bfloat16
    )
    q_latent = collect(q_part, SEQ, 2)
    first_slot = lax.axis_index(SEQ) * slots_dev
    page_count = (lengths + page_len - 1) // page_len
    logical = jnp.arange(page_table.shape[1], dtype=jnp.int32)
    live_page = logical[None, :] < page_count[:, None]
    tokens_in = jnp.clip(lengths[:, None] - page_len * logical[None, :], 0, page_len)
    local_ids = jnp.arange(slots_dev, dtype=jnp.int32)
    hits = ((page_table - first_slot)[:, :, None] == local_ids[None, None, :]) & live_page[
        :, :, None
    ]
    owner_mask = jnp.any(hits, axis=1)
    slot_fill = jnp.sum(jnp.where(hits, tokens_in[:, :, None], 0), axis=(0, 1))
    owner_half = owner_mask.astype(jnp.bfloat16)

    def update(run_state, index):
        run_max, run_sum, run_out = run_state
        start = index * 8
        latent_block = lax.dynamic_slice_in_dim(latent_cache, start, 8, 0)
        rope_block = lax.dynamic_slice_in_dim(rope_cache, start, 8, 0).reshape(
            8, page_len, rope_width
        )
        owner_block = lax.dynamic_slice_in_dim(owner_half, start, 8, 1)
        fill_block = lax.dynamic_slice_in_dim(slot_fill, start, 8, 0)
        pick_latent = jnp.einsum(
            "bs,bhk->shk", owner_block, q_latent, preferred_element_type=jnp.float32
        ).astype(jnp.bfloat16)
        pick_rope = jnp.einsum(
            "bs,bhr->shr", owner_block, q_rope, preferred_element_type=jnp.float32
        ).astype(jnp.bfloat16)
        scores = (
            jnp.einsum(
                "shk,stk->sht", pick_latent, latent_block, preferred_element_type=jnp.float32
            )
            + jnp.einsum("shr,str->sht", pick_rope, rope_block, preferred_element_type=jnp.float32)
        ) * score_scale
        live_token = (
            jnp.arange(page_len, dtype=jnp.int32)[None, None, :] < fill_block[:, None, None]
        )
        slot_max = jnp.max(jnp.where(live_token, scores, NEG), axis=2)
        exponent = jnp.where(live_token, jnp.exp(scores - slot_max[:, :, None]), 0.0)
        slot_sum = jnp.sum(exponent, axis=2)
        slot_out = jnp.einsum(
            "sht,stk->shk",
            exponent.astype(jnp.bfloat16),
            latent_block,
            preferred_element_type=jnp.float32,
        )
        owned = owner_block > 0
        candidate = jnp.where(owned[:, :, None], slot_max[None, :, :], NEG)
        new_max = jnp.maximum(run_max, jnp.max(candidate, axis=1))
        carry_scale = jnp.exp(run_max - new_max)
        factor = jnp.where(owned[:, :, None], jnp.exp(candidate - new_max[:, None, :]), 0.0)
        run_sum = run_sum * carry_scale + jnp.einsum("bsh,sh->bh", factor, slot_sum)
        run_out = run_out * carry_scale[:, :, None] + jnp.einsum("bsh,shk->bhk", factor, slot_out)
        return (new_max, run_sum, run_out)

    def visit(index, run_state):
        return update(run_state, index)

    initial = (
        jnp.full((seq_count, heads), NEG, jnp.float32),
        jnp.zeros((seq_count, heads), jnp.float32),
        jnp.zeros((seq_count, heads, latent_width), jnp.float32),
    )
    run_max, run_sum, run_out = lax.fori_loop(0, slots_dev // 8, visit, initial)
    share_width = value_up_weight.shape[1]
    shards = lax.axis_size(SEQ)
    spread_max = jnp.broadcast_to(run_max[:, :, None], (seq_count, heads, shards))
    spread_sum = jnp.broadcast_to(run_sum[:, :, None], (seq_count, heads, shards))
    peers_max, peers_sum, peers_out = (
        *side_by_side((spread_max, spread_sum), SEQ, 2, 2, 0),
        lax.all_to_all(run_out, SEQ, split_axis=2, concat_axis=2, tiled=True),
    )
    top = jnp.max(peers_max, axis=2)
    rescale = jnp.exp(peers_max - top[:, :, None])
    totals = jnp.sum(peers_sum * rescale, axis=2)
    grouped = peers_out.reshape(seq_count, heads, shards, share_width)
    shared_latent = jnp.sum(grouped * rescale[:, :, :, None], axis=2)
    local_portion = (shared_latent / totals[:, :, None]).astype(jnp.bfloat16)
    value_slice = jnp.einsum(
        "gre,req->grq", local_portion, value_up_weight, preferred_element_type=jnp.float32
    )
    value_rows = by_axis(value_slice, SEQ).astype(jnp.bfloat16)
    flat_values = value_rows.reshape(seq_count, heads * value_rows.shape[2])
    partial_out = jnp.dot(flat_values, w_out, preferred_element_type=jnp.float32)
    return sum_at_owner(partial_out, "mp", 1).astype(jnp.bfloat16)


def solution(mesh):
    finer = Mesh(
        mesh.devices.reshape(mesh.shape["groups"], 8, 8, mesh.shape["mp"]),
        ("groups", "seq_0", "seq_1", "mp"),
    )
    return jax.shard_map(
        local,
        mesh=finer,
        in_specs=(
            P(GROUPS_SEQ, None, None),
            P(GROUPS_SEQ, None),
            P("groups", "mp", None),
            P("groups", "mp", None),
            P("mp", None, SEQ),
            P("mp", SEQ, None),
            P("mp", SEQ),
            P("groups", None),
            P("groups"),
        ),
        out_specs=P("groups", SEQ_MP),
        check_vma=False,
    )
```

profile of v0, /device:TPU:513, one launch (start us, length us, event | category | flops | bytes accessed | tf_op | source)
XLA Modules:
  0.0 388.7 jit_solution(2890915873763073449)
XLA Ops:
  9.8 21.8 %all-to-all-start = ((bf16[64,2,2048]{2,1,0:T(2,128)(2,1)}), bf16[64,2,2048]{2,1,0:T(2,128)(2,1)}, u32[]{:S(2)}, u32[]{:S(2)}) async-start(bf16[64,2,2048]{2,1,0:T(2,128)(2,1)} %reshape.114), calls=%async_computation | async-start | bytes 1048576 | tf_op jit(solution)/shard_map/all_to_all | solution.py:23
  31.9 5.7 %fusion.41 = pred[8,128]{1,0:T(8,128)(4,1)S(1)} fusion(s32[8,2048]{1,0:T(8,128)S(1)} %get-tuple-element.269, pred[8,2048]{1,0:T(8,128)(4,1)S(1)} %iota_compare_fusion.2), kind=kLoop, calls=%fused_computation.56 | loop fusion | flops 6290432 | bytes 82944 | tf_op jit(solution)/shard_map/reduce_or | solution.py:83
  37.7 7.8 %select_reduce_fusion.2 = s32[128]{0:T(128)S(1)} fusion(s32[8,2048]{1,0:T(8,128)S(1)} %get-tuple-element.268, s32[8,2048]{1,0:T(8,128)S(1)} %get-tuple-element.269, pred[8,2048]{1,0:T(8,128)(4,1)S(1)} %iota_compare_fusion.2), kind=kLoop, calls=%fused_computation.53 | loop fusion | flops 8388480 | bytes 147968 | tf_op jit(solution)/shard_map/reduce_sum | solution.py:84
  51.0 138.7 %while.18 = (s32[]{:T(128)}, f32[8,64]{0,1:T(8,128)S(1)}, f32[8,64]{0,1:T(8,128)S(1)}, f32[8,64,512]{2,0,1:T(8,128)}, bf16[8,128]{1,0:T(8,128)(2,1)S(1)}, /*inde...) while((s32[]{:T(128)}, f32[8,64]{0,1:T(8,128)S(1)}, ...), condition=%wide.region_6.7_spmd.clone, body=%wide.region_2.6_spmd.clone.sunk | while | flops 81668672 | bytes 7003699 | solution.py:137
  64.5 2.7 fusion.94
  73.3 2.7 fusion.94
  82.0 2.7 fusion.94
  90.8 2.7 fusion.94
  99.5 2.7 fusion.94
  117.0 2.7 fusion.94
  125.7 2.7 fusion.94
  143.2 2.7 fusion.94
  151.9 2.7 fusion.94
  160.7 2.7 fusion.94
  169.4 2.7 fusion.94
  190.9 13.3 %all-to-all-start.2 = ((f32[64,1,1024]{2,1,0:T(1,128)}), f32[64,1,1024]{2,1,0:T(1,128)S(1)}, u32[]{:S(2)}, u32[]{:S(2)}) async-start(f32[64,1,1024]{2,1,0:T(1,128)} %reshape.118), calls=%async_computation.2 | async-start | bytes 524288 | tf_op jit(solution)/shard_map/all_to_all | solution.py:38
  206.6 3.4 reshape.116
  210.0 5.1 %all-to-all-done.2 = f32[64,1,1024]{2,1,0:T(1,128)S(1)} async-done(((f32[64,1,1024]{2,1,0:T(1,128)}), f32[64,1,1024]{2,1,0:T(1,128)S(1)}, u32[]{:S(2)}, u32[]{:S(2)}) %all-to-all-start.2) | async-done | bytes 262176 | tf_op jit(solution)/shard_map/all_to_all | solution.py:38
  215.2 7.9 %all-to-all-start.1 = ((f32[64,1,4096]{2,1,0:T(1,128)}), f32[64,1,4096]{2,1,0:T(1,128)}, u32[]{:S(2)}, u32[]{:S(2)}) async-start(f32[64,1,4096]{2,1,0:T(1,128)} %reshape.116), calls=%async_computation.1 | async-start | bytes 2097152 | tf_op jit(solution)/shard_map/all_to_all | solution.py:144
  225.3 18.9 %all-to-all-done.1 = f32[64,1,4096]{2,1,0:T(1,128)} async-done(((f32[64,1,4096]{2,1,0:T(1,128)}), f32[64,1,4096]{2,1,0:T(1,128)}, u32[]{:S(2)}, u32[]{:S(2)}) %all-to-all-start.1) | async-done | bytes 1048608 | tf_op jit(solution)/shard_map/all_to_all | solution.py:144
  244.2 4.4 %reduce = f32[64,4096]{1,0:T(8,128)S(1)} reduce(f32[64,1,4096]{2,1,0:T(1,128)} %all-to-all-done.1, f32[]{:T(128)} %broadcast.134), dimensions={1}, to_apply=%all_to_all.13.reduce_sub_computation | reduce | bytes 2097156 | tf_op jit(solution)/shard_map/all_to_all | solution.py:144
  254.1 82.6 %all-reduce.3.cloned.1.call-done = f32[8,64,128]{2,0,1:T(8,128)} async-done(((f32[8,64,128]{2,0,1:T(8,128)}), f32[8,64,128]{2,0,1:T(8,128)}) %all-reduce.3.cloned.1.call-update) | async-done | bytes 262160 | tf_op jit(solution)/shard_map/psum | solution.py:47
  336.7 26.8 %all-reduce.4 = bf16[8,64,128]{2,0,1:T(8,128)(2,1)S(1)} all-reduce(f32[8,64,128]{2,0,1:T(8,128)} %all-reduce.3.cloned.1.call-done), channel_id=1, replica_groups=mesh['groups'=2,'seq_0'=8,'seq_1'=8,'mp'=2] {'seq_1'}, use_global_device_ids=true, to_apply=%region_11.12 | all-reduce | flops 65536 | bytes 393216 | tf_op jit(solution)/shard_map/psum | solution.py:47
  364.5 16.0 %all_to_all.20 = f32[2,1,448]{2,1,0:T(1,128)S(1)} all-to-all(f32[2,1,448]{2,1,0:T(1,128)S(1)} %reshape.120), channel_id=1, replica_groups=mesh['groups'=2,'seq_0'=8,'seq_1'=8,'mp'=2] {'mp'}, dimensions={0} | all-to-all | bytes 7168 | tf_op jit(solution)/shard_map/all_to_all | solution.py:59
  (395 shorter events, 130.1 us)
Async XLA Ops:
  6.5 356.9 %copy-start = (bf16[8192,112]{0,1:T(8,128)(2,1)S(1)}, bf16[8192,112]{0,1:T(8,128)(2,1)}, u32[]{:S(2)}) copy-start(bf16[8192,112]{0,1:T(8,128)(2,1)} %param.17) | copy-start | bytes 5505028
  6.6 25.2 %copy-start.5 = (s32[8]{0:T(128)S(1)}, s32[8]{0:T(128)}, u32[]{:S(2)}) copy-start(s32[8]{0:T(128)} %param.19) | copy-start | bytes 100
  6.6 25.2 %copy-start.4 = (s32[8,2048]{1,0:T(8,128)S(1)}, s32[8,2048]{1,0:T(8,128)}, u32[]{:S(2)}) copy-start(s32[8,2048]{1,0:T(8,128)} %param.18) | copy-start | bytes 196612
  7.9 29.8 %copy-start.2 = (bf16[8,64,64]{2,1,0:T(8,128)(2,1)S(1)}, bf16[8,64,64]{2,1,0:T(8,128)(2,1)}, u32[]{:S(2)}) copy-start(bf16[8,64,64]{2,1,0:T(8,128)(2,1)} %param.14) | copy-start | bytes 196612
  9.8 35.7 %all-to-all-start = ((bf16[64,2,2048]{2,1,0:T(2,128)(2,1)}), bf16[64,2,2048]{2,1,0:T(2,128)(2,1)}, u32[]{:S(2)}, u32[]{:S(2)}) async-start(bf16[64,2,2048]{2,1,0:T(2,128)(2,1)} %reshape.114), calls=%async_computation | async-start | bytes 1048576 | tf_op jit(solution)/shard_map/all_to_all | solution.py:23
  189.6 14.6 %copy-start.1 = (f32[8,64,512]{2,0,1:T(8,128)S(1)}, f32[8,64,512]{2,0,1:T(8,128)}, u32[]{:S(2)}) copy-start(f32[8,64,512]{2,0,1:T(8,128)} %get-tuple-element.176) | copy-start | bytes 3145732
  190.9 24.2 %all-to-all-start.2 = ((f32[64,1,1024]{2,1,0:T(1,128)}), f32[64,1,1024]{2,1,0:T(1,128)S(1)}, u32[]{:S(2)}, u32[]{:S(2)}) async-start(f32[64,1,1024]{2,1,0:T(1,128)} %reshape.118), calls=%async_computation.2 | async-start | bytes 524288 | tf_op jit(solution)/shard_map/all_to_all | solution.py:38
  215.2 29.0 %all-to-all-start.1 = ((f32[64,1,4096]{2,1,0:T(1,128)}), f32[64,1,4096]{2,1,0:T(1,128)}, u32[]{:S(2)}, u32[]{:S(2)}) async-start(f32[64,1,4096]{2,1,0:T(1,128)} %reshape.116), calls=%async_computation.1 | async-start | bytes 2097152 | tf_op jit(solution)/shard_map/all_to_all | solution.py:144
  223.1 113.6 %all-reduce.3.cloned.1.call-start = ((), (), s32[]{:S(2)}) async-start(), calls=%async_computation.4 | async-start | bytes 524288 | tf_op jit(solution)/shard_map/psum | solution.py:47
  248.5 4.5 %copy-start.3 = (bf16[64,8,128]{2,1,0:T(8,128)(2,1)S(1)}, bf16[64,8,128]{2,1,0:T(8,128)(2,1)}, u32[]{:S(2)}) copy-start(bf16[64,8,128]{2,1,0:T(8,128)(2,1)} %param.16) | copy-start | bytes 393220
Sparse Core Ops, SparseCore 0:
  254.2 82.4 all-reduce.2
where the time goes:
time: 392 us; the launch traced here: 389 us
  matrix products  110 us (28%)
  waiting for transfers between devices  107 us (27%)
  starting transfers between devices  43.1 us (11%)
  blocking collectives  42.8 us (11%)
  local copies, waits for them, and re-layouts  42.3 us (11%)
  other arithmetic  29.5 us (8%)
  between operations  13.7 us (3%)
    psum x1, waiting for transfers between devices, by_axis(): x = lax.psum(x, axis)  82.6 us
    dot_general x16, matrix products, update(): jnp.einsum('bsh,shk->bhk', factor, slot_out)  42.6 us
    psum x1, blocking collectives, by_axis(): x = lax.psum(x, axis)  26.8 us
    dot_general x16, matrix products, update(): jnp.einsum('sht,stk->shk', exponent.astype(jnp.bfloat16), latent_block, p...  24.3 us
    dot_general x16, matrix products, update(): jnp.einsum('shk,stk->sht', pick_latent, latent_block, preferred_element_t...  22 us
    all_to_all x1, starting transfers between devices, from_everyone(): lax.all_to_all(jnp.broadcast_to(x[None], (size, *x.shape)), axis, 0, 0, t...  21.8 us
    all_to_all x1, waiting for transfers between devices, local(): lax.all_to_all(run_out, SEQ, split_axis=2, concat_axis=2, tiled=True)  18.9 us
    all_to_all x1, blocking collectives, sum_at_owner(): tiles = lax.all_to_all(cut_along(x, dim, size), axis, 0, 0, tiled=True)  16 us
  transfers between devices with their start and end apart: 4, of which 3 were waited for; matrix products, arithmetic and copies ran while one was open for 6% of the time, Pallas kernels for 0%

commit v1 on v0

v1 whole, which is shorter than its diff:
```python
import functools
import math

import jax
import jax.numpy as jnp
from jax import lax
from jax.experimental import pallas as pl
from jax.experimental.pallas import tpu as pltpu
from jax.sharding import PartitionSpec as P

GROUPS_SEQ = ("groups", "seq")
NEG = -1e30
F32 = jnp.float32
BF16 = jnp.bfloat16
NT = (((1,), (1,)), ((), ()))
NN = (((1,), (0,)), ((), ()))


def dot(a, b, dims):
    return lax.dot_general(a, b, dims, preferred_element_type=F32)


def kernel(
    side,
    scale,
    q_nope,
    q_rope,
    w_uk,
    w_up,
    table,
    lengths,
    latent_hbm,
    rope_hbm,
    w_out_hbm,
    out,
    lat,
    rope,
    wout,
    spread,
    keys,
    q_all,
    g0,
    g1,
    wb1,
    wb2,
    fills,
    owner_v,
    owner_s,
    sc,
    mrow,
    lrow,
    probs,
    acc,
    mtile,
    mx,
    mt2,
    my,
    ltile,
    lx,
    lt2,
    ly,
    sx,
    sy,
    rx,
    ry,
    stage,
    r0,
    r1,
    s2y,
    s2x,
    r2y,
    r2x,
    vals,
    part_send,
    part_recv,
    load_sem,
    own_sem,
    send_sem,
    recv_sem,
    mp_sem,
):
    seqs, heads, nope = q_nope.shape
    slots, page, width = lat.shape
    half = seqs * heads // 2
    hw = width // 2
    me = lax.axis_index("seq")
    mp = lax.axis_index("mp")
    x, y = lax.div(me, side), lax.rem(me, side)
    hops = sorted(range(1, side), key=lambda k: -min(k, side - k))

    def to_x(k):
        return lax.rem(x + k, side)

    def to_y(k):
        return lax.rem(y + k, side)

    def at_x(k):
        return {"seq": to_x(k) * side + y}

    def at_y(k):
        return {"seq": x * side + to_y(k)}

    loads = []
    n_cut = 4
    cut = slots // n_cut

    def load(src, dst):
        copy = pltpu.make_async_copy(src, dst, load_sem.at[len(loads)])
        copy.start()
        loads.append(copy)

    load(rope_hbm, rope)
    for i in range(n_cut):
        load(latent_hbm.at[pl.ds(i * cut, cut)], lat.at[pl.ds(i * cut, cut)])
    load(w_out_hbm, wout)

    barrier = pltpu.get_barrier_semaphore()
    for k in hops:
        pl.semaphore_signal(barrier, inc=1, device_id=at_x(k), device_id_type=pl.DeviceIdType.MESH)
        pl.semaphore_signal(barrier, inc=1, device_id=at_y(k), device_id_type=pl.DeviceIdType.MESH)
    pl.semaphore_signal(
        barrier, inc=1, device_id={"mp": 1 - mp}, device_id_type=pl.DeviceIdType.MESH
    )

    started = []

    def send(phase, k, src, dst, device):
        copy = pltpu.make_async_remote_copy(
            src_ref=src,
            dst_ref=dst,
            send_sem=send_sem.at[phase, k],
            recv_sem=recv_sem.at[phase, k],
            device_id=device,
            device_id_type=pl.DeviceIdType.MESH,
        )
        copy.start()
        started.append(copy)
        return copy

    def arrive(copies):
        for copy in copies:
            copy.wait_recv()

    cols = w_uk.shape[1]
    wide = dot(
        w_uk[...].reshape(heads * cols, nope), q_nope[...].reshape(seqs * heads, nope), NT
    ).reshape(heads, cols, seqs * heads)
    row_head = lax.broadcasted_iota(jnp.int32, wide.shape, 0)
    col_head = lax.rem(lax.broadcasted_iota(jnp.int32, wide.shape, 2), heads)
    q_part = jnp.sum(jnp.where(row_head == col_head, wide, 0.0), axis=0).astype(BF16)
    g0[x, y] = q_part[:, :half]
    g1[y, x] = q_part[:, half:]

    pl.semaphore_wait(barrier, 2 * (side - 1) + 1)

    first0 = [send(0, k, g0.at[x, y], g0.at[x, y], at_y(k)) for k in hops]
    first1 = [send(1, k, g1.at[y, x], g1.at[y, x], at_x(k)) for k in hops]

    lane = lax.broadcasted_iota(jnp.int32, (1, 128), 1)
    low = lane < page
    pitch = spread.shape[0] // slots
    rope_copy, lat_copies, wout_copy = loads[0], loads[1:-1], loads[-1]
    rope_copy.wait()

    def spread_pair(c, carry):
        z = rope[:, pl.ds(pl.multiple_of(c * 128, 128), 128)].astype(F32)
        spread[pl.ds(2 * c, slots, stride=pitch), :] = jnp.where(low, z, 0.0)
        spread[pl.ds(2 * c + 1, slots, stride=pitch), :] = jnp.where(low, 0.0, z)
        return carry

    lax.fori_loop(0, rope.shape[1] // 128, spread_pair, 0)

    arrive(first0)
    arrive(first1)
    second0 = [send(2, k, g0.at[x], g0.at[x], at_x(k)) for k in hops]
    second1 = [send(3, k, g1.at[y], g1.at[y], at_y(k)) for k in hops]
    up1 = [
        send(4, k, w_up.at[pl.ds(to_x(k) * side, side)], wb1.at[x], at_x(k)) for k in hops
    ]
    wb1[x] = w_up[pl.ds(x * side, side)]

    def pack_rows(s, carry):
        keys[pl.ds(pl.multiple_of(s * page, page), page), :] = spread[
            pl.ds(s * pitch, page), :
        ].astype(BF16)
        return carry

    lax.fori_loop(0, slots, pack_rows, 0, unroll=4)

    def owner_of(slot):
        return jnp.clip(owner_s[0, slot], 0, seqs - 1)

    row = lax.broadcasted_iota(jnp.int32, (seqs, 1), 0)
    length = jnp.zeros((seqs, 1), jnp.int32)
    for b in range(seqs):
        length = jnp.where(row == b, lengths[b], length)
    pages = lax.broadcasted_iota(jnp.int32, table.shape, 1)
    tokens = jnp.clip(length - page * pages, 0, page).astype(F32)
    relative = table[...] - me * slots
    lane8 = lax.broadcasted_iota(jnp.int32, (seqs, 128), 1)
    token = lax.rem(lane8, page).astype(F32)

    def fill_pair(i, owner):
        f0 = jnp.max(jnp.where(relative == 2 * i, tokens, 0.0), axis=1, keepdims=True)
        f1 = jnp.max(jnp.where(relative == 2 * i + 1, tokens, 0.0), axis=1, keepdims=True)
        fills[i] = jnp.where(lane8 < page, f0, f1) - token
        owner = jnp.where((lane8 == 2 * i) & (f0 > 0.0), row, owner)
        return jnp.where((lane8 == 2 * i + 1) & (f1 > 0.0), row, owner)

    owner = lax.fori_loop(
        0, slots // 2, fill_pair, jnp.zeros((seqs, 128), jnp.int32), unroll=2
    )
    owner_v[...] = jnp.broadcast_to(
        jnp.max(owner.astype(F32), axis=0, keepdims=True), owner.shape
    ).astype(jnp.int32)
    own_copy = pltpu.make_async_copy(owner_v, owner_s, own_sem)
    own_copy.start()

    for b in range(seqs):
        q_all[b, :, width:] = jnp.concatenate([q_rope[b], q_rope[b]], axis=-1)

    arrive(up1)
    up2 = [send(5, k, wb1.at[:, to_y(k)], wb2.at[:, y], at_y(k)) for k in hops]
    wb2[:, y] = wb1[:, y]
    own_copy.wait()
    arrive(second0)
    arrive(second1)

    eye = (
        lax.broadcasted_iota(jnp.int32, (half, half), 0)
        == lax.broadcasted_iota(jnp.int32, (half, half), 1)
    ).astype(BF16)
    columns0 = g0[...].reshape(width, half)
    columns1 = jnp.concatenate(
        [g1[:, i].reshape(side * cols, half) for i in range(side)], axis=0
    )
    for i, columns in enumerate((columns0, columns1)):
        rows = dot(eye, columns, NT).astype(BF16).reshape(seqs // 2, heads, width)
        q_all[i * (seqs // 2) : (i + 1) * (seqs // 2), :, :width] = rows

    for copy in lat_copies:
        copy.wait()

    def score_group(g, carry):
        picked = jnp.concatenate([q_all[owner_of(4 * g + j)] for j in range(4)], axis=0)
        tok = lat[pl.ds(g * 4, 4)].reshape(4 * page, width)
        rot = keys[pl.ds(pl.multiple_of(g * 4 * page, 4 * page), 4 * page), :]
        s = dot(picked[:, :width], tok, NT) + dot(picked[:, width:], rot, NT)
        for j in range(2):
            r, c = 2 * heads * j, 2 * page * j
            sc[2 * g + j] = jnp.where(
                low,
                s[r : r + heads, c : c + 2 * page],
                s[r + heads : r + 2 * heads, c : c + 2 * page],
            )
        return carry

    lax.fori_loop(0, slots // 4, score_group, 0)

    n_pairs = slots // 2
    for b in range(0, seqs, 2):

        def pair_max(i, carry):
            m0, m1 = carry
            s = sc[i]
            m0 = jnp.maximum(m0, jnp.where(fills[i, b : b + 1] > 0.0, s, NEG))
            m1 = jnp.maximum(m1, jnp.where(fills[i, b + 1 : b + 2] > 0.0, s, NEG))
            return m0, m1

        start = jnp.full((heads, 128), NEG, F32)
        m0, m1 = lax.fori_loop(0, n_pairs, pair_max, (start, start), unroll=4)
        for d, m in enumerate((m0, m1)):
            mrow[b + d] = jnp.broadcast_to(jnp.max(m, axis=1, keepdims=True), (heads, 128))

    head_lane = lax.broadcasted_iota(jnp.int32, (heads, 128), 1)
    head_row = lax.broadcasted_iota(jnp.int32, (heads, 128), 0)
    diag = head_lane == head_row

    def to_lanes(ref):
        return jnp.concatenate(
            [
                jnp.sum(jnp.where(diag, ref[b], 0.0), axis=0, keepdims=True)
                for b in range(seqs)
            ],
            axis=0,
        )

    mtile[...] = to_lanes(mrow)
    max1 = [send(6, k, mtile, mx.at[x], at_x(k)) for k in hops]

    factor = scale * math.log2(math.e)
    n_chunks = 4
    per = n_pairs // n_chunks
    acc[...] = jnp.zeros(acc.shape, F32)
    lrow[...] = jnp.zeros(lrow.shape, F32)
    for c in range(n_chunks):

        def weigh(i, carry):
            i = c * per + i
            top = jnp.where(low, mrow[owner_of(2 * i)], mrow[owner_of(2 * i + 1)])
            live = jnp.max(fills[i], axis=0, keepdims=True) > 0.0
            sc[i] = jnp.where(live, jnp.exp2((sc[i] - top) * factor), 0.0)
            return carry

        lax.fori_loop(0, per, weigh, 0, unroll=2)
        for b in range(seqs):

            def place(i, total):
                p = jnp.where(fills[c * per + i, b : b + 1] > 0.0, sc[c * per + i], 0.0)
                probs[
                    b * heads : (b + 1) * heads, pl.ds(pl.multiple_of(i * 128, 128), 128)
                ] = p.astype(BF16)
                return total + p

            lrow[b] = lax.fori_loop(0, per, place, lrow[b], unroll=4)
        n_tok = per * 2
        acc[...] += dot(
            probs[...], lat[c * n_tok : (c + 1) * n_tok].reshape(n_tok * page, width), NN
        )
        if c == 1:
            arrive(max1)
            top = mtile[...]
            for k in hops:
                top = jnp.maximum(top, mx[to_x(k)])
            mt2[...] = top
            max2 = [send(7, k, mt2, my.at[y], at_y(k)) for k in hops]

    arrive(max2)
    top = mt2[...]
    for k in hops:
        top = jnp.maximum(top, my[to_y(k)])

    tiles = hw // 128

    def every(ref, start, count):
        return jnp.concatenate(
            [ref[t, pl.ds(start, count, stride=side), :] for t in range(tiles)], axis=1
        ).astype(BF16)

    def put(ref, b, rows):
        for t in range(tiles):
            ref[t, b * side : (b + 1) * side, :] = rows[:, 128 * t : 128 * (t + 1)]

    for b in range(seqs):
        above = jnp.sum(
            jnp.where(diag, jnp.broadcast_to(top[b : b + 1], (heads, 128)), 0.0),
            axis=1,
            keepdims=True,
        )
        f = jnp.exp2((mrow[b] - above) * factor)
        lrow[b] = f * jnp.sum(lrow[b], axis=1, keepdims=True)
        rows = acc[b * heads : (b + 1) * heads, :] * f[:, :1]
        for t in range(tiles):
            stage[t, b * heads : (b + 1) * heads, :] = rows[
                :, hw + 128 * t : hw + 128 * (t + 1)
            ]
        sx[:, b] = rows[:, :hw].astype(BF16).reshape(side, side, hw)
    sum1 = [send(8, k, sx.at[to_x(k)], rx.at[x], at_x(k)) for k in hops]
    for b in range(seqs):
        for i in range(side):
            sy[i, b] = every(stage, b * heads + i, side)
    sum2 = [send(9, k, sy.at[to_y(k)], ry.at[y], at_y(k)) for k in hops]
    ltile[...] = to_lanes(lrow)
    tot1 = [send(10, k, ltile, lx.at[x], at_x(k)) for k in hops]

    arrive(sum1)
    for b in range(seqs):
        rows = sx[x, b].astype(F32)
        for k in hops:
            rows += rx[to_x(k), b].astype(F32)
        put(r0, b, rows)
    for i in range(side):
        s2y[i] = every(r0, i, seqs)
    fin1 = [send(11, k, s2y.at[to_y(k)], r2y.at[y], at_y(k)) for k in hops]
    arrive(sum2)
    for b in range(seqs):
        rows = sy[y, b].astype(F32)
        for k in hops:
            rows += ry[to_y(k), b].astype(F32)
        put(r1, b, rows)
    for i in range(side):
        s2x[i] = every(r1, i, seqs)
    fin2 = [send(12, k, s2x.at[to_x(k)], r2x.at[x], at_x(k)) for k in hops]
    arrive(tot1)
    total = ltile[...]
    for k in hops:
        total += lx[to_x(k)]
    lt2[...] = total
    tot2 = [send(13, k, lt2, ly.at[y], at_y(k)) for k in hops]

    arrive(fin1)
    att0 = s2y[y].astype(F32)
    for k in hops:
        att0 += r2y[to_y(k)].astype(F32)
    arrive(fin2)
    att1 = s2x[x].astype(F32)
    for k in hops:
        att1 += r2x[to_x(k)].astype(F32)
    arrive(tot2)
    total = lt2[...]
    for k in hops:
        total += ly[to_y(k)]
    total = jnp.sum(jnp.where(lane8 == me, total, 0.0), axis=1, keepdims=True)
    attention = (jnp.concatenate([att0, att1], axis=1) / total).astype(BF16)

    arrive(up2)
    value = dot(attention, wb2[...].reshape(width, wb2.shape[-1]), NN).astype(BF16)
    vals[x, y] = value
    val1 = [send(14, k, vals.at[x, y], vals.at[x, y], at_y(k)) for k in hops]
    wout_copy.wait()
    arrive(val1)
    val2 = [send(15, k, vals.at[x], vals.at[x], at_x(k)) for k in hops]
    arrive(val2)
    flat = jnp.concatenate(
        [vals[i, j] for i in range(side) for j in range(side)], axis=1
    )
    partial = dot(flat, wout[...], NT)
    width_out = partial.shape[1]
    part_send[:, :width_out] = partial
    swap = pltpu.make_async_remote_copy(
        src_ref=part_send,
        dst_ref=part_recv,
        send_sem=mp_sem.at[0],
        recv_sem=mp_sem.at[1],
        device_id={"mp": 1 - mp},
        device_id_type=pl.DeviceIdType.MESH,
    )
    swap.start()
    swap.wait()
    both = partial + part_recv[:, :width_out]
    n_out = out.shape[1]
    out[...] = jnp.where(mp == 0, both[:, :n_out], both[:, n_out:]).astype(BF16)
    for copy in started:
        copy.wait_send()


def local(
    latent_cache, rope_cache, q_nope, q_rope, w_uk, value_up_weight, w_out, page_table, lengths
):
    slots, page, width = latent_cache.shape
    seqs, heads, nope = q_nope.shape
    cols, vdim = value_up_weight.shape[1:]
    side = math.isqrt(lax.axis_size("seq"))
    scale = (nope + q_rope.shape[2]) ** (-0.5)
    n_out = w_out.shape[1] // lax.axis_size("mp")
    half = seqs * heads // 2
    hw = width // 2
    chunk = slots * page // 4
    pitch = page + 4
    vm = pltpu.VMEM
    anywhere = pl.BlockSpec(memory_space=pl.ANY)
    in_vmem = pl.BlockSpec(memory_space=pltpu.VMEM)
    scratch = [
        vm((slots, page, width), BF16),
        vm(rope_cache.shape, BF16),
        vm((w_out.shape[1], w_out.shape[0]), BF16),
        vm((slots * pitch + page, 128), F32),
        vm((slots * page, 128), BF16),
        vm((seqs, heads, width + 128), BF16),
        vm((side, side, cols, half), BF16),
        vm((side, side, cols, half), BF16),
        vm((side, side, cols, vdim), BF16),
        vm((side, side, cols, vdim), BF16),
        vm((slots // 2, seqs, 128), F32),
        vm((seqs, 128), jnp.int32),
        pltpu.SMEM((seqs, 128), jnp.int32),
        vm((slots // 2, heads, 128), F32),
        vm((seqs, heads, 128), F32),
        vm((seqs, heads, 128), F32),
        vm((seqs * heads, chunk), BF16),
        vm((seqs * heads, width), F32),
        vm((seqs, 128), F32),
        vm((side, seqs, 128), F32),
        vm((seqs, 128), F32),
        vm((side, seqs, 128), F32),
        vm((seqs, 128), F32),
        vm((side, seqs, 128), F32),
        vm((seqs, 128), F32),
        vm((side, seqs, 128), F32),
        vm((side, seqs, side, hw), BF16),
        vm((side, seqs, side, hw), BF16),
        vm((side, seqs, side, hw), BF16),
        vm((side, seqs, side, hw), BF16),
        vm((hw // 128, seqs * heads + side, 128), F32),
        vm((hw // 128, seqs * side + side, 128), F32),
        vm((hw // 128, seqs * side + side, 128), F32),
        vm((side, seqs, hw), BF16),
        vm((side, seqs, hw), BF16),
        vm((side, seqs, hw), BF16),
        vm((side, seqs, hw), BF16),
        vm((side, side, seqs, vdim), BF16),
        vm((seqs, 128), F32),
        vm((seqs, 128), F32),
        pltpu.SemaphoreType.DMA((6,)),
        pltpu.SemaphoreType.DMA,
        pltpu.SemaphoreType.DMA((16, side)),
        pltpu.SemaphoreType.DMA((16, side)),
        pltpu.SemaphoreType.DMA((2,)),
    ]
    return pl.pallas_call(
        functools.partial(kernel, side, scale),
        out_shape=jax.ShapeDtypeStruct((seqs, n_out), BF16),
        in_specs=[in_vmem] * 5
        + [pl.BlockSpec(memory_space=pltpu.SMEM)]
        + [anywhere] * 3,
        out_specs=in_vmem,
        scratch_shapes=scratch,
        compiler_params=pltpu.CompilerParams(
            collective_id=0, has_side_effects=True, vmem_limit_bytes=60 * 1024 * 1024
        ),
        name="decode",
    )(
        q_nope,
        q_rope,
        jnp.swapaxes(w_uk, 1, 2),
        value_up_weight,
        page_table,
        lengths,
        latent_cache,
        rope_cache,
        jnp.swapaxes(w_out, 0, 1),
    )


def solution(mesh):
    return jax.shard_map(
        local,
        mesh=mesh,
        in_specs=(
            P(GROUPS_SEQ, None, None),
            P(GROUPS_SEQ, None),
            P("groups", "mp", None),
            P("groups", "mp", None),
            P("mp", None, "seq"),
            P("mp", "seq", None),
            P("mp", "seq"),
            P("groups", None),
            P("groups"),
        ),
        out_specs=P("groups", ("seq", "mp")),
        check_vma=False,
    )
```

time: 392 us -> 86.9 us (0.22)
  matrix products: 110 us -> 0 us
  waiting for transfers between devices: 107 us -> 0 us
  Pallas kernels: 0 us -> 85.5 us
  starting transfers between devices: 43.1 us -> 0 us
  blocking collectives: 42.8 us -> 0 us
  local copies, waits for them, and re-layouts: 42.3 us -> 1.26 us
  other arithmetic: 29.5 us -> 0 us
  between operations: 13.7 us -> 0.01 us
    dot_general x115 -> x0, matrix products: 110 us -> none  [the longest x16 42.6 us: update(): jnp.einsum('bsh,shk->bhk', factor, slot_out)]
    pallas_call x0 -> x1, Pallas kernels: none -> 85.5 us  [local(): pl.pallas_call(functools.partial(kernel, side, scale), out_shape=jax.Shap...]
    psum x1 -> x0, waiting for transfers between devices: 82.6 us -> none  [by_axis(): x = lax.psum(x, axis)]
    all_to_all x3 -> x0, starting transfers between devices: 43 us -> none  [the longest x1 21.8 us: from_everyone(): lax.all_to_all(jnp.broadcast_to(x[None], (size, *x.shape)), axis, 0, 0, t...]
    psum x1 -> x0, blocking collectives: 26.8 us -> none  [by_axis(): x = lax.psum(x, axis)]
    all_to_all x3 -> x0, waiting for transfers between devices: 24 us -> none  [the longest x1 18.9 us: local(): lax.all_to_all(run_out, SEQ, split_axis=2, concat_axis=2, tiled=True)]
    dynamic_slice x64 -> x0, local copies, waits for them, and re-layouts: 17.3 us -> none  [the longest x16 13.5 us: update(): lax.dynamic_slice_in_dim(rope_cache, start, 8, 0)]
    all_to_all x1 -> x0, blocking collectives: 16 us -> none  [sum_at_owner(): tiles = lax.all_to_all(cut_along(x, dim, size), axis, 0, 0, tiled=True)]
  transfers between devices with their start and end apart: 4 -> 0, of which waited for: 3 -> 0; matrix products, arithmetic and copies ran while one was open for 6% -> 0% of each run, Pallas kernels for 0% -> 0%
where the time goes in v1:
time: 86.9 us; the launch traced here: 86.8 us
  Pallas kernels  85.5 us (98%)
  local copies, waits for them, and re-layouts  1.26 us (1%)
    pallas_call x1, Pallas kernels, local(): pl.pallas_call(functools.partial(kernel, side, scale), out_shape=jax.Shap...  85.5 us

profile of v1, /device:TPU:513, one launch (start us, length us, event | category | flops | bytes accessed | tf_op | source)
XLA Modules:
  0.0 86.8 jit_solution(9213481511634184356)
XLA Ops:
  0.0 85.5 %decode.1 = bf16[8,56]{1,0:T(8,128)(2,1)} custom-call(bf16[8,64,128]{2,1,0:T(8,128)(2,1)} %q_nope.1, bf16[8,64,64]{2,1,0:T(8,128)(2,1)} %q_rope.1, bf16[64,8,128]{2,1,0:T(8,128)(2,1)} %bitcast.3, bf16[64,8,128]{2,1,0:T(8,128)(2,1)} %w_up.1, s32[8,2048]{1,0:T(8,128)} %table.1, s32[8]{0:T(128)} %lengths.1, bf16[128,64,512]{2,1,0:T(8,128)(2,1)} %latent_hbm.1, ...), custom_call_target="tpu_custom_call" | custom-call | tf_op jit(solution)/shard_map/decode/pallas_call | solution.py:500
  85.5 1.3 %copy.11 = bf16[8,56]{1,0:T(8,128)(2,1)} copy(bf16[8,56]{1,0:T(8,128)(2,1)} %decode.1) | data formatting | bytes 1792

commit v2 on v1

--- a/solution.py
+++ b/solution.py
@@ -49,12 +49,16 @@
     sc,
     mrow,
     lrow,
+    mrun,
     probs,
     acc,
+    maskt,
+    maskl,
     mtile,
     mx,
     mt2,
     my,
+    my2,
     ltile,
     lx,
     lt2,
@@ -170,23 +174,6 @@
 
     lax.fori_loop(0, rope.shape[1] // 128, spread_pair, 0)
 
-    arrive(first0)
-    arrive(first1)
-    second0 = [send(2, k, g0.at[x], g0.at[x], at_x(k)) for k in hops]
-    second1 = [send(3, k, g1.at[y], g1.at[y], at_y(k)) for k in hops]
-    up1 = [
-        send(4, k, w_up.at[pl.ds(to_x(k) * side, side)], wb1.at[x], at_x(k)) for k in hops
-    ]
-    wb1[x] = w_up[pl.ds(x * side, side)]
-
-    def pack_rows(s, carry):
-        keys[pl.ds(pl.multiple_of(s * page, page), page), :] = spread[
-            pl.ds(s * pitch, page), :
-        ].astype(BF16)
-        return carry
-
-    lax.fori_loop(0, slots, pack_rows, 0, unroll=4)
-
     def owner_of(slot):
         return jnp.clip(owner_s[0, slot], 0, seqs - 1)
 
@@ -208,7 +195,7 @@
         return jnp.where((lane8 == 2 * i + 1) & (f1 > 0.0), row, owner)
 
     owner = lax.fori_loop(
-        0, slots // 2, fill_pair, jnp.zeros((seqs, 128), jnp.int32), unroll=2
+        0, slots // 2, fill_pair, jnp.zeros((seqs, 128), jnp.int32), unroll=8
     )
     owner_v[...] = jnp.broadcast_to(
         jnp.max(owner.astype(F32), axis=0, keepdims=True), owner.shape
@@ -216,15 +203,38 @@
     own_copy = pltpu.make_async_copy(owner_v, owner_s, own_sem)
     own_copy.start()
 
+    arrive(first0)
+    arrive(first1)
+    second0 = [send(2, k, g0.at[x], g0.at[x], at_x(k)) for k in hops]
+    second1 = [send(3, k, g1.at[y], g1.at[y], at_y(k)) for k in hops]
+    def pack_rows(s, carry):
+        keys[pl.ds(pl.multiple_of(s * page, page), page), :] = spread[
+            pl.ds(s * pitch, page), :
+        ].astype(BF16)
+        return carry
+
+    lax.fori_loop(0, slots, pack_rows, 0, unroll=4)
+
+    def mask_pair(i, carry):
+        live = jnp.where(fills[i] > 0.0, 1.0, 0.0)
+        maskl[i] = live.astype(BF16)
+        for b in range(seqs):
+            maskt[i, b] = jnp.broadcast_to(live[b : b + 1], (16, 128)).astype(BF16)
+        return carry
+
+    lax.fori_loop(0, slots // 2, mask_pair, 0, unroll=4)
+
     for b in range(seqs):
         q_all[b, :, width:] = jnp.concatenate([q_rope[b], q_rope[b]], axis=-1)
 
-    arrive(up1)
-    up2 = [send(5, k, wb1.at[:, to_y(k)], wb2.at[:, y], at_y(k)) for k in hops]
-    wb2[:, y] = wb1[:, y]
     own_copy.wait()
     arrive(second0)
     arrive(second1)
+
+    up1 = [
+        send(4, k, w_up.at[pl.ds(to_x(k) * side, side)], wb1.at[x], at_x(k)) for k in hops
+    ]
+    wb1[x] = w_up[pl.ds(x * side, side)]
 
     eye = (
         lax.broadcasted_iota(jnp.int32, (half, half), 0)
@@ -246,31 +256,27 @@
         tok = lat[pl.ds(g * 4, 4)].reshape(4 * page, width)
         rot = keys[pl.ds(pl.multiple_of(g * 4 * page, 4 * page), 4 * page), :]
         s = dot(picked[:, :width], tok, NT) + dot(picked[:, width:], rot, NT)
+        blocks = []
         for j in range(2):
             r, c = 2 * heads * j, 2 * page * j
-            sc[2 * g + j] = jnp.where(
+            block = jnp.where(
                 low,
                 s[r : r + heads, c : c + 2 * page],
                 s[r + heads : r + 2 * heads, c : c + 2 * page],
             )
+            sc[2 * g + j] = block
+            blocks.append(block)
+        for b in range(seqs):
+            m = mrun[b]
+            for j in range(2):
+                m = jnp.maximum(m, jnp.where(fills[2 * g + j, b : b + 1] > 0.0, blocks[j], NEG))
+            mrun[b] = m
         return carry
 
-    lax.fori_loop(0, slots // 4, score_group, 0)
-
-    n_pairs = slots // 2
-    for b in range(0, seqs, 2):
-
-        def pair_max(i, carry):
-            m0, m1 = carry
-            s = sc[i]
-            m0 = jnp.maximum(m0, jnp.where(fills[i, b : b + 1] > 0.0, s, NEG))
-            m1 = jnp.maximum(m1, jnp.where(fills[i, b + 1 : b + 2] > 0.0, s, NEG))
-            return m0, m1
-
-        start = jnp.full((heads, 128), NEG, F32)
-        m0, m1 = lax.fori_loop(0, n_pairs, pair_max, (start, start), unroll=4)
-        for d, m in enumerate((m0, m1)):
-            mrow[b + d] = jnp.broadcast_to(jnp.max(m, axis=1, keepdims=True), (heads, 128))
+    mrun[...] = jnp.full(mrun.shape, NEG, F32)
+    lax.fori_loop(0, slots // 4, score_group, 0, unroll=8)
+    for b in range(seqs):
+        mrow[b] = jnp.broadcast_to(jnp.max(mrun[b], axis=1, keepdims=True), (heads, 128))
 
     head_lane = lax.broadcasted_iota(jnp.int32, (heads, 128), 1)
     head_row = lax.broadcasted_iota(jnp.int32, (heads, 128), 0)
@@ -287,48 +293,46 @@
 
     mtile[...] = to_lanes(mrow)
     max1 = [send(6, k, mtile, mx.at[x], at_x(k)) for k in hops]
+    max1y = [send(7, k, mtile, my.at[y], at_y(k)) for k in hops]
+    arrive(up1)
+    up2 = [send(5, k, wb1.at[:, to_y(k)], wb2.at[:, y], at_y(k)) for k in hops]
+    wb2[:, y] = wb1[:, y]
 
     factor = scale * math.log2(math.e)
+    n_pairs = slots // 2
     n_chunks = 4
     per = n_pairs // n_chunks
-    acc[...] = jnp.zeros(acc.shape, F32)
-    lrow[...] = jnp.zeros(lrow.shape, F32)
+    n_tok = per * 2
+    lsum = jnp.zeros((heads, seqs), F32)
     for c in range(n_chunks):
-
-        def weigh(i, carry):
-            i = c * per + i
+        for j in range(per):
+            i = c * per + j
             top = jnp.where(low, mrow[owner_of(2 * i)], mrow[owner_of(2 * i + 1)])
             live = jnp.max(fills[i], axis=0, keepdims=True) > 0.0
-            sc[i] = jnp.where(live, jnp.exp2((sc[i] - top) * factor), 0.0)
-            return carry
-
-        lax.fori_loop(0, per, weigh, 0, unroll=2)
-        for b in range(seqs):
-
-            def place(i, total):
-                p = jnp.where(fills[c * per + i, b : b + 1] > 0.0, sc[c * per + i], 0.0)
-                probs[
-                    b * heads : (b + 1) * heads, pl.ds(pl.multiple_of(i * 128, 128), 128)
-                ] = p.astype(BF16)
-                return total + p
-
-            lrow[b] = lax.fori_loop(0, per, place, lrow[b], unroll=4)
-        n_tok = per * 2
-        acc[...] += dot(
+            p = jnp.where(live, jnp.exp2((sc[i] - top) * factor), 0.0).astype(BF16)
+            p16 = p.reshape(heads // 16, 16, 128)
+            for b in range(seqs):
+                probs[b * heads : (b + 1) * heads, j * 128 : (j + 1) * 128] = (
+                    p16 * maskt[i, b][None]
+                ).reshape(heads, 128)
+            lsum += dot(p, maskl[i], NT)
+        part = dot(
             probs[...], lat[c * n_tok : (c + 1) * n_tok].reshape(n_tok * page, width), NN
         )
-        if c == 1:
+        acc[...] = part if c == 0 else acc[...] + part
+        if c == 2:
             arrive(max1)
-            top = mtile[...]
+            top_x = mtile[...]
             for k in hops:
-                top = jnp.maximum(top, mx[to_x(k)])
-            mt2[...] = top
-            max2 = [send(7, k, mt2, my.at[y], at_y(k)) for k in hops]
-
-    arrive(max2)
-    top = mt2[...]
-    for k in hops:
-        top = jnp.maximum(top, my[to_y(k)])
+                top_x = jnp.maximum(top_x, mx[to_x(k)])
+            mt2[...] = top_x
+            max2 = [send(16, k, mt2, my2.at[y], at_y(k)) for k in hops]
+
+    arrive(max1y)
+    top_x = mt2[...]
+    top_y = mtile[...]
+    for k in hops:
+        top_y = jnp.maximum(top_y, my[to_y(k)])
 
     tiles = hw // 128
 
@@ -341,20 +345,24 @@
         for t in range(tiles):
             ref[t, b * side : (b + 1) * side, :] = rows[:, 128 * t : 128 * (t + 1)]
 
-    for b in range(seqs):
-        above = jnp.sum(
-            jnp.where(diag, jnp.broadcast_to(top[b : b + 1], (heads, 128)), 0.0),
+    def column(tile, b):
+        return jnp.sum(
+            jnp.where(diag, jnp.broadcast_to(tile[b : b + 1], (heads, 128)), 0.0),
             axis=1,
             keepdims=True,
         )
-        f = jnp.exp2((mrow[b] - above) * factor)
-        lrow[b] = f * jnp.sum(lrow[b], axis=1, keepdims=True)
-        rows = acc[b * heads : (b + 1) * heads, :] * f[:, :1]
+
+    for b in range(seqs):
+        local_top = mrow[b]
+        f0 = jnp.exp2((local_top - column(top_x, b)) * factor)
+        f1 = jnp.exp2((local_top - column(top_y, b)) * factor)
+        lrow[b] = f0 * lsum[:, b : b + 1]
+        rows = acc[b * heads : (b + 1) * heads, :]
+        sx[:, b] = (rows[:, :hw] * f0[:, :1]).astype(BF16).reshape(side, side, hw)
         for t in range(tiles):
-            stage[t, b * heads : (b + 1) * heads, :] = rows[
-                :, hw + 128 * t : hw + 128 * (t + 1)
-            ]
-        sx[:, b] = rows[:, :hw].astype(BF16).reshape(side, side, hw)
+            stage[t, b * heads : (b + 1) * heads, :] = (
+                rows[:, hw + 128 * t : hw + 128 * (t + 1)] * f1
+            )
     sum1 = [send(8, k, sx.at[to_x(k)], rx.at[x], at_x(k)) for k in hops]
     for b in range(seqs):
         for i in range(side):
@@ -363,12 +371,28 @@
     ltile[...] = to_lanes(lrow)
     tot1 = [send(10, k, ltile, lx.at[x], at_x(k)) for k in hops]
 
+    arrive(max2)
+    top = top_x
+    for k in hops:
+        top = jnp.maximum(top, my2[to_y(k)])
+    shrink_x = jnp.exp2((top_x - top) * factor)
+    shrink_y = jnp.exp2((top_y - top) * factor)
+    row8 = lax.broadcasted_iota(jnp.int32, (side, 128), 0)
+    lane_of = lax.broadcasted_iota(jnp.int32, (side, 128), 1)
+
+    def pick(tile, b, which):
+        return jnp.sum(
+            jnp.where(lane_of == which, jnp.broadcast_to(tile[b : b + 1], (side, 128)), 0.0),
+            axis=1,
+            keepdims=True,
+        )
+
     arrive(sum1)
     for b in range(seqs):
         rows = sx[x, b].astype(F32)
         for k in hops:
             rows += rx[to_x(k), b].astype(F32)
-        put(r0, b, rows)
+        put(r0, b, rows * pick(shrink_x, b, x * side + row8))
     for i in range(side):
         s2y[i] = every(r0, i, seqs)
     fin1 = [send(11, k, s2y.at[to_y(k)], r2y.at[y], at_y(k)) for k in hops]
@@ -377,7 +401,7 @@
         rows = sy[y, b].astype(F32)
         for k in hops:
             rows += ry[to_y(k), b].astype(F32)
-        put(r1, b, rows)
+        put(r1, b, rows * pick(shrink_y, b, row8 * side + y))
     for i in range(side):
         s2x[i] = every(r1, i, seqs)
     fin2 = [send(12, k, s2x.at[to_x(k)], r2x.at[x], at_x(k)) for k in hops]
@@ -385,7 +409,7 @@
     total = ltile[...]
     for k in hops:
         total += lx[to_x(k)]
-    lt2[...] = total
+    lt2[...] = total * shrink_x
     tot2 = [send(13, k, lt2, ly.at[y], at_y(k)) for k in hops]
 
     arrive(fin1)
@@ -467,11 +491,15 @@
         vm((slots // 2, heads, 128), F32),
         vm((seqs, heads, 128), F32),
         vm((seqs, heads, 128), F32),
+        vm((seqs, heads, 128), F32),
         vm((seqs * heads, chunk), BF16),
         vm((seqs * heads, width), F32),
+        vm((slots // 2, seqs, 16, 128), BF16),
+        vm((slots // 2, seqs, 128), BF16),
         vm((seqs, 128), F32),
         vm((side, seqs, 128), F32),
         vm((seqs, 128), F32),
+        vm((side, seqs, 128), F32),
         vm((side, seqs, 128), F32),
         vm((seqs, 128), F32),
         vm((side, seqs, 128), F32),
@@ -493,8 +521,8 @@
         vm((seqs, 128), F32),
         pltpu.SemaphoreType.DMA((6,)),
         pltpu.SemaphoreType.DMA,
-        pltpu.SemaphoreType.DMA((16, side)),
-        pltpu.SemaphoreType.DMA((16, side)),
+        pltpu.SemaphoreType.DMA((17, side)),
+        pltpu.SemaphoreType.DMA((17, side)),
         pltpu.SemaphoreType.DMA((2,)),
     ]
     return pl.pallas_call(

time: 86.9 us -> 77 us (0.89)
  Pallas kernels: 85.5 us -> 75.6 us
    pallas_call x1, Pallas kernels: 85.5 us -> 75.6 us  [local(): pl.pallas_call(functools.partial(kernel, side, scale), out_shape=jax.Shap...]
where the time goes in v2:
time: 77 us; the launch traced here: 76.9 us
  Pallas kernels  75.6 us (98%)
  local copies, waits for them, and re-layouts  1.26 us (2%)
    pallas_call x1, Pallas kernels, local(): pl.pallas_call(functools.partial(kernel, side, scale), out_shape=jax.Shap...  75.6 us

profile of v2, /device:TPU:513, one launch (start us, length us, event | category | flops | bytes accessed | tf_op | source)
XLA Modules:
  0.0 76.9 jit_solution(734506067899354941)
XLA Ops:
  0.0 75.6 %decode.1 = bf16[8,56]{1,0:T(8,128)(2,1)} custom-call(bf16[8,64,128]{2,1,0:T(8,128)(2,1)} %q_nope.1, bf16[8,64,64]{2,1,0:T(8,128)(2,1)} %q_rope.1, bf16[64,8,128]{2,1,0:T(8,128)(2,1)} %bitcast.3, bf16[64,8,128]{2,1,0:T(8,128)(2,1)} %w_up.1, s32[8,2048]{1,0:T(8,128)} %table.1, s32[8]{0:T(128)} %lengths.1, bf16[128,64,512]{2,1,0:T(8,128)(2,1)} %latent_hbm.1, ...), custom_call_target="tpu_custom_call" | custom-call | tf_op jit(solution)/shard_map/decode/pallas_call | solution.py:528
  75.6 1.3 %copy.11 = bf16[8,56]{1,0:T(8,128)(2,1)} copy(bf16[8,56]{1,0:T(8,128)(2,1)} %decode.1) | data formatting | bytes 1792

commit v3 on v2

--- a/solution.py
+++ b/solution.py
@@ -23,16 +23,22 @@
 def kernel(
     side,
     scale,
+    q_nope_hbm,
+    q_rope_hbm,
+    w_uk_hbm,
+    w_up_hbm,
+    table_hbm,
+    lengths_hbm,
+    latent_hbm,
+    rope_hbm,
+    w_out_hbm,
+    out,
     q_nope,
     q_rope,
     w_uk,
     w_up,
     table,
     lengths,
-    latent_hbm,
-    rope_hbm,
-    w_out_hbm,
-    out,
     lat,
     rope,
     wout,
@@ -104,20 +110,6 @@
     def at_y(k):
         return {"seq": x * side + to_y(k)}
 
-    loads = []
-    n_cut = 4
-    cut = slots // n_cut
-
-    def load(src, dst):
-        copy = pltpu.make_async_copy(src, dst, load_sem.at[len(loads)])
-        copy.start()
-        loads.append(copy)
-
-    load(rope_hbm, rope)
-    for i in range(n_cut):
-        load(latent_hbm.at[pl.ds(i * cut, cut)], lat.at[pl.ds(i * cut, cut)])
-    load(w_out_hbm, wout)
-
     barrier = pltpu.get_barrier_semaphore()
     for k in hops:
         pl.semaphore_signal(barrier, inc=1, device_id=at_x(k), device_id_type=pl.DeviceIdType.MESH)
@@ -125,6 +117,26 @@
     pl.semaphore_signal(
         barrier, inc=1, device_id={"mp": 1 - mp}, device_id_type=pl.DeviceIdType.MESH
     )
+
+    loads = []
+    n_cut = 4
+    cut = slots // n_cut
+
+    def load(src, dst):
+        copy = pltpu.make_async_copy(src, dst, load_sem.at[len(loads)])
+        copy.start()
+        loads.append(copy)
+        return copy
+
+    query_copies = [load(q_nope_hbm, q_nope), load(w_uk_hbm, w_uk)]
+    rope_copy = load(rope_hbm, rope)
+    table_copies = [load(table_hbm, table), load(lengths_hbm, lengths)]
+    side_copies = [load(q_rope_hbm, q_rope), load(w_up_hbm, w_up)]
+    lat_copies = [
+        load(latent_hbm.at[pl.ds(i * cut, cut)], lat.at[pl.ds(i * cut, cut)])
+        for i in range(n_cut)
+    ]
+    wout_copy = load(w_out_hbm, wout)
 
     started = []
 
@@ -145,6 +157,9 @@
         for copy in copies:
             copy.wait_recv()
 
+    for copy in query_copies:
+        copy.wait()
+
     cols = w_uk.shape[1]
     wide = dot(
         w_uk[...].reshape(heads * cols, nope), q_nope[...].reshape(seqs * heads, nope), NT
@@ -157,13 +172,33 @@
 
     pl.semaphore_wait(barrier, 2 * (side - 1) + 1)
 
-    first0 = [send(0, k, g0.at[x, y], g0.at[x, y], at_y(k)) for k in hops]
-    first1 = [send(1, k, g1.at[y, x], g1.at[y, x], at_x(k)) for k in hops]
+    near = hops[::-1]
+    first0 = {k: send(0, k, g0.at[x, y], g0.at[x, y], at_y(k)) for k in hops}
+    first1 = {k: send(1, k, g1.at[y, x], g1.at[y, x], at_x(k)) for k in hops}
+
+    def forward(phase, k, piece, device):
+        return pltpu.make_async_remote_copy(
+            src_ref=piece,
+            dst_ref=piece,
+            send_sem=send_sem.at[phase, k],
+            recv_sem=recv_sem.at[phase, k],
+            device_id=device,
+            device_id_type=pl.DeviceIdType.MESH,
+        )
+
+    def pass_on(row, col):
+        for k in hops:
+            forward(2, k, g0.at[x, row], at_x(k)).start()
+            forward(3, k, g1.at[y, col], at_y(k)).start()
+
+    second0 = [forward(2, k, g0.at[x], at_x(k)) for k in hops]
+    second1 = [forward(3, k, g1.at[y], at_y(k)) for k in hops]
+    started.extend(second0 + second1)
+    pass_on(y, x)
 
     lane = lax.broadcasted_iota(jnp.int32, (1, 128), 1)
     low = lane < page
     pitch = spread.shape[0] // slots
-    rope_copy, lat_copies, wout_copy = loads[0], loads[1:-1], loads[-1]
     rope_copy.wait()
 
     def spread_pair(c, carry):
@@ -176,6 +211,9 @@
 
     def owner_of(slot):
         return jnp.clip(owner_s[0, slot], 0, seqs - 1)
+
+    for copy in table_copies:
+        copy.wait()
 
     row = lax.broadcasted_iota(jnp.int32, (seqs, 1), 0)
     length = jnp.zeros((seqs, 1), jnp.int32)
@@ -203,10 +241,10 @@
     own_copy = pltpu.make_async_copy(owner_v, owner_s, own_sem)
     own_copy.start()
 
-    arrive(first0)
-    arrive(first1)
-    second0 = [send(2, k, g0.at[x], g0.at[x], at_x(k)) for k in hops]
-    second1 = [send(3, k, g1.at[y], g1.at[y], at_y(k)) for k in hops]
+    for k in near:
+        first0[k].wait_recv()
+        first1[k].wait_recv()
+        pass_on(to_y(side - k), to_x(side - k))
     def pack_rows(s, carry):
         keys[pl.ds(pl.multiple_of(s * page, page), page), :] = spread[
             pl.ds(s * pitch, page), :
@@ -224,6 +262,8 @@
 
     lax.fori_loop(0, slots // 2, mask_pair, 0, unroll=4)
 
+    for copy in side_copies:
+        copy.wait()
     for b in range(seqs):
         q_all[b, :, width:] = jnp.concatenate([q_rope[b], q_rope[b]], axis=-1)
 
@@ -353,17 +393,18 @@
         )
 
     for b in range(seqs):
-        local_top = mrow[b]
-        f0 = jnp.exp2((local_top - column(top_x, b)) * factor)
-        f1 = jnp.exp2((local_top - column(top_y, b)) * factor)
+        f0 = jnp.exp2((mrow[b] - column(top_x, b)) * factor)
         lrow[b] = f0 * lsum[:, b : b + 1]
-        rows = acc[b * heads : (b + 1) * heads, :]
-        sx[:, b] = (rows[:, :hw] * f0[:, :1]).astype(BF16).reshape(side, side, hw)
+        rows = acc[b * heads : (b + 1) * heads, :hw] * f0[:, :1]
+        sx[:, b] = rows.astype(BF16).reshape(side, side, hw)
+    sum1 = [send(8, k, sx.at[to_x(k)], rx.at[x], at_x(k)) for k in hops]
+    for b in range(seqs):
+        f1 = jnp.exp2((mrow[b] - column(top_y, b)) * factor)
+        rows = acc[b * heads : (b + 1) * heads, hw:]
         for t in range(tiles):
             stage[t, b * heads : (b + 1) * heads, :] = (
-                rows[:, hw + 128 * t : hw + 128 * (t + 1)] * f1
+                rows[:, 128 * t : 128 * (t + 1)] * f1
             )
-    sum1 = [send(8, k, sx.at[to_x(k)], rx.at[x], at_x(k)) for k in hops]
     for b in range(seqs):
         for i in range(side):
             sy[i, b] = every(stage, b * heads + i, side)
@@ -433,12 +474,18 @@
     val1 = [send(14, k, vals.at[x, y], vals.at[x, y], at_y(k)) for k in hops]
     wout_copy.wait()
     arrive(val1)
-    val2 = [send(15, k, vals.at[x], vals.at[x], at_x(k)) for k in hops]
-    arrive(val2)
-    flat = jnp.concatenate(
-        [vals[i, j] for i in range(side) for j in range(side)], axis=1
-    )
-    partial = dot(flat, wout[...], NT)
+    val2 = {k: send(15, k, vals.at[x], vals.at[x], at_x(k)) for k in hops}
+    block = side * vals.shape[-1]
+
+    def project(i):
+        flat = jnp.concatenate([vals[i, j] for j in range(side)], axis=1)
+        start = pl.multiple_of(i * block, block)
+        return dot(flat, wout[:, pl.ds(start, block)], NT)
+
+    partial = project(x)
+    for k in near:
+        val2[k].wait_recv()
+        partial += project(to_x(side - k))
     width_out = partial.shape[1]
     part_send[:, :width_out] = partial
     swap = pltpu.make_async_remote_copy(
@@ -475,6 +522,12 @@
     anywhere = pl.BlockSpec(memory_space=pl.ANY)
     in_vmem = pl.BlockSpec(memory_space=pltpu.VMEM)
     scratch = [
+        vm(q_nope.shape, BF16),
+        vm(q_rope.shape, BF16),
+        vm((heads, cols, nope), BF16),
+        vm(value_up_weight.shape, BF16),
+        vm(page_table.shape, jnp.int32),
+        pltpu.SMEM(lengths.shape, jnp.int32),
         vm((slots, page, width), BF16),
         vm(rope_cache.shape, BF16),
         vm((w_out.shape[1], w_out.shape[0]), BF16),
@@ -519,7 +572,7 @@
         vm((side, side, seqs, vdim), BF16),
         vm((seqs, 128), F32),
         vm((seqs, 128), F32),
-        pltpu.SemaphoreType.DMA((6,)),
+        pltpu.SemaphoreType.DMA((12,)),
         pltpu.SemaphoreType.DMA,
         pltpu.SemaphoreType.DMA((17, side)),
         pltpu.SemaphoreType.DMA((17, side)),
@@ -528,9 +581,7 @@
     return pl.pallas_call(
         functools.partial(kernel, side, scale),
         out_shape=jax.ShapeDtypeStruct((seqs, n_out), BF16),
-        in_specs=[in_vmem] * 5
-        + [pl.BlockSpec(memory_space=pltpu.SMEM)]
-        + [anywhere] * 3,
+        in_specs=[anywhere] * 9,
         out_specs=in_vmem,
         scratch_shapes=scratch,
         compiler_params=pltpu.CompilerParams(

time: 77 us -> 74.3 us (0.965)
  Pallas kernels: 75.6 us -> 72.9 us
    pallas_call x1, Pallas kernels: 75.6 us -> 72.9 us  [local(): pl.pallas_call(functools.partial(kernel, side, scale), out_shape=jax.Shap...]
where the time goes in v3:
time: 74.3 us; the launch traced here: 74.2 us
  Pallas kernels  72.9 us (98%)
  local copies, waits for them, and re-layouts  1.26 us (2%)
    pallas_call x1, Pallas kernels, local(): pl.pallas_call(functools.partial(kernel, side, scale), out_shape=jax.Shap...  72.9 us

profile of v3, /device:TPU:513, one launch (start us, length us, event | category | flops | bytes accessed | tf_op | source)
XLA Modules:
  0.0 74.2 jit_solution(4797019556673207835)
XLA Ops:
  0.0 72.9 %decode.1 = bf16[8,56]{1,0:T(8,128)(2,1)} custom-call(bf16[8,64,128]{2,1,0:T(8,128)(2,1)} %q_nope_hbm.1, bf16[8,64,64]{2,1,0:T(8,128)(2,1)} %q_rope_hbm.1, bf16[64,8,128]{2,1,0:T(8,128)(2,1)} %bitcast.3, bf16[64,8,128]{2,1,0:T(8,128)(2,1)} %w_up_hbm.1, s32[8,2048]{1,0:T(8,128)} %table_hbm.1, s32[8]{0:T(128)} %lengths_hbm.1, ...), custom_call_target="tpu_custom_call" | custom-call | tf_op jit(solution)/shard_map/decode/pallas_call | solution.py:581
  72.9 1.3 %copy.11 = bf16[8,56]{1,0:T(8,128)(2,1)} copy(bf16[8,56]{1,0:T(8,128)(2,1)} %decode.1) | data formatting | bytes 1792

commit v4 on v3

--- a/solution.py
+++ b/solution.py
@@ -580,7 +580,7 @@
     ]
     return pl.pallas_call(
         functools.partial(kernel, side, scale),
-        out_shape=jax.ShapeDtypeStruct((seqs, n_out), BF16),
+        out_shape=pltpu.VMEM((seqs, n_out), BF16),
         in_specs=[anywhere] * 9,
         out_specs=in_vmem,
         scratch_shapes=scratch,

time: 74.3 us -> 73 us (0.983)
  no operation moved by 1% of the time
where the time goes in v4:
time: 73 us; the launch traced here: 72.9 us
  Pallas kernels  72.3 us (99%)
    pallas_call x1, Pallas kernels, local(): pl.pallas_call(functools.partial(kernel, side, scale), out_shape=pltpu.VM...  72.3 us

profile of v4, /device:TPU:513, one launch (start us, length us, event | category | flops | bytes accessed | tf_op | source)
XLA Modules:
  0.0 72.9 jit_solution(13762213913341260108)
XLA Ops:
  0.0 72.3 %decode.1 = bf16[8,56]{1,0:T(8,128)(2,1)S(1)} custom-call(bf16[8,64,128]{2,1,0:T(8,128)(2,1)} %q_nope_hbm.1, bf16[8,64,64]{2,1,0:T(8,128)(2,1)} %q_rope_hbm.1, bf16[64,8,128]{2,1,0:T(8,128)(2,1)} %bitcast.3, bf16[64,8,128]{2,1,0:T(8,128)(2,1)} %w_up_hbm.1, s32[8,2048]{1,0:T(8,128)} %table_hbm.1, s32[8]{0:T(128)} %lengths_hbm.1, ...), custom_call_target="tpu_custom_call" | custom-call | tf_op jit(solution)/shard_map/decode/pallas_call | solution.py:581
  72.3 0.6 copy.11
